TPU v7x, 256 devices: a whole 4x4x8 slice. The times are simulated.
256 devices in a mesh: bank: 16 (over y, x), zero: 16 (over z, core).
Axes of the slice: x: 4, y: 4, z: 8, core: 2. Of those that a mesh axis runs over, the one named last changes fastest.
Arguments:
- w_down: float32 [64, 1024, 2048], P('bank', None, 'zero'), may hold values from -0.25 to 0.25
- avg_down: bfloat16 [64, 1024, 2048], P('bank', None, 'zero'), may hold values from -0.09375 to 0.09375
- router_weight: float32 [2048, 64], P('zero', 'bank'), may hold values from -0.125 to 0.125
- router_gain: float32 [2048], P('zero'), may hold values from 0.25 to 1.75
Outputs:
- serve_down: bfloat16 [64, 1024, 2048], P('bank')
- scale_down: float32 [64, 1024], P('bank')
- serve_router: bfloat16 [2048, 64], replicated
All inputs are finite; a program needn't handle non-finite values.
Results may differ from a plain program's by a relative error of at most 0.001.
Values may be sent and summed in bfloat16 or wider, within the bound.
No kernel may reach another device: no remote copies, remote signals or barrier semaphores. Data moves between devices by JAX's collectives and lax.ppermute only.
A program may use at most 128 MiB of HBM per device.

v0:
```python
import jax
import jax.numpy as jnp
from jax import lax
from jax.sharding import PartitionSpec as P


def copy_for_each(x, axis):
    copies = jnp.broadcast_to(x, (lax.axis_size(axis), *x.shape))
    return lax.all_to_all(copies, axis, split_axis=0, concat_axis=0, tiled=True)


def over_copies(x, axis):
    return copy_for_each(x, axis).sum(axis=0)


def in_order(parts, dim):
    dims = list(parts.shape[1:])
    dims[dim] *= parts.shape[0]
    return jnp.moveaxis(parts, 0, dim).reshape(dims)


def gather_directly(x, axis, dim):
    parts = copy_for_each(x, axis)
    return in_order(parts, dim)


def shards(w_down, avg_down, router_weight, router_gain):
    fresh_down = w_down + avg_down.astype(jnp.float32)
    total_down = over_copies(jnp.sum(fresh_down * fresh_down, axis=2), "zero")
    scale_down = jnp.sqrt(total_down)
    narrow_down = (fresh_down / jnp.expand_dims(scale_down, 2)).astype(jnp.bfloat16)
    serve_down = lax.all_gather(narrow_down, "zero", axis=2, tiled=True)
    part_router = (router_weight * router_gain[:, None]).astype(jnp.bfloat16)
    row_router = gather_directly(part_router, "zero", 0)
    serve_router = gather_directly(row_router, "bank", 1)
    return (serve_down, scale_down, serve_router)


def solution(mesh):
    return jax.shard_map(
        shards,
        mesh=mesh,
        in_specs=(P("bank", None, "zero"), P("bank", None, "zero"), P("zero", "bank"), P("zero")),
        out_specs=(P("bank", None, None), P("bank", None), P()),
        check_vma=False,
    )
```

profile of v0, /device:TPU:1, one launch (start us, length us, event | category | flops | bytes accessed | tf_op | source)
XLA Modules:
  0.0 152.9 jit_solution(14177765800500866044)
XLA Ops:
  7.2 0.0 copy-start
  7.2 0.0 copy-start.1
  7.2 0.0 all-gather.2.cloned.1.call-start
  7.2 2.6 %multiply_reduce_fusion = f32[4,1024]{1,0:T(4,128)S(1)} fusion(f32[4,1024,128]{2,1,0:T(8,128)} %param.4, bf16[4,1024,128]{2,1,0:T(8,128)(2,1)} %param.5), kind=kLoop, calls=%fused_computation.1 | loop fusion | flops 2093056 | bytes 3162112 | tf_op jit(solution)/shard_map/reduce_sum | solution.py:29
  9.9 21.4 %all_to_all.15 = f32[16,4,1024]{2,1,0:T(4,128)S(1)} all-to-all(f32[16,4,1024]{2,1,0:T(4,128)S(1)} %broadcast_in_dim.11), channel_id=1, replica_groups=mesh['bank'=16,'zero'=16] {'zero'}, dimensions={0} | all-to-all | bytes 524288 | tf_op jit(solution)/shard_map/all_to_all | solution.py:9
  31.3 0.1 reduce_sum.19
  31.3 0.0 copy-done
  31.4 0.0 copy-done.1
  31.4 0.0 copy-start.2
  31.4 0.0 copy-start.3
  31.4 0.0 copy-start.4
  31.4 1.5 divide_convert_fusion
  32.9 0.0 copy-done.2
  32.9 0.0 all-gather.2.cloned.1.call-update
  32.9 0.0 copy-done.3
  33.0 0.0 copy-done.4
  33.0 10.1 %all_to_all.16 = bf16[16,128,4]{1,2,0:T(4,128)(2,1)S(1)} all-to-all(bf16[16,128,4]{1,2,0:T(4,128)(2,1)S(1)} %broadcast_in_dim.12), channel_id=1, replica_groups=mesh['bank'=16,'zero'=16] {'zero'}, dimensions={0} | all-to-all | bytes 32768 | tf_op jit(solution)/shard_map/all_to_all | solution.py:9
  43.1 0.1 broadcast_in_dim.13
  43.2 14.7 %all_to_all.17 = bf16[16,2048,4]{1,2,0:T(4,128)(2,1)S(1)} all-to-all(bf16[16,2048,4]{1,2,0:T(4,128)(2,1)S(1)} %broadcast_in_dim.13), channel_id=1, replica_groups=mesh['bank'=16,'zero'=16] {'bank'}, dimensions={0} | all-to-all | bytes 524288 | tf_op jit(solution)/shard_map/all_to_all | solution.py:9
  57.9 0.8 reshape.17
  58.6 73.3 %all-gather.2.cloned.1.call-done = bf16[4,1024,2048]{2,1,0:T(8,128)(2,1)} async-done(((bf16[4,1024,128]{2,1,0:T(8,128)(2,1)}), bf16[4,1024,2048]{2,1,0:T(8,128)(2,1)}) %all-gather.2.cloned.1.call-update) | async-done | bytes 16777232 | tf_op jit(solution)/shard_map/all_gather | solution.py:32
  131.9 14.2 %copy.10 = bf16[4,1024,2048]{2,1,0:T(8,128)(2,1)} copy(bf16[4,1024,2048]{2,1,0:T(8,128)(2,1)} %all-gather.2.cloned.1.call-done) | data formatting | bytes 33554432
  (4 shorter events, 0.1 us)
Async XLA Ops:
  7.2 24.2 %copy-start = (f32[4,1024,128]{2,1,0:T(8,128)S(1)}, f32[4,1024,128]{2,1,0:T(8,128)}, u32[]{:S(2)}) copy-start(f32[4,1024,128]{2,1,0:T(8,128)} %param.4) | copy-start | bytes 6291460
  7.2 24.2 %copy-start.1 = (bf16[4,1024,128]{2,1,0:T(8,128)(2,1)S(1)}, bf16[4,1024,128]{2,1,0:T(8,128)(2,1)}, u32[]{:S(2)}) copy-start(bf16[4,1024,128]{2,1,0:T(8,128)(2,1)} %param.5) | copy-start | bytes 3145732
  7.2 124.7 %all-gather.2.cloned.1.call-start = ((), (), s32[]{:S(2)}) async-start(), calls=%async_computation.3 | async-start | bytes 17825792 | tf_op jit(solution)/shard_map/all_gather | solution.py:32
  31.4 1.6 %copy-start.2 = (f32[4,1024]{1,0:T(4,128)}, f32[4,1024]{1,0:T(4,128)S(1)}, u32[]{:S(2)}) copy-start(f32[4,1024]{1,0:T(4,128)S(1)} %sqrt.7) | copy-start | bytes 49156
  31.4 1.6 %copy-start.3 = (f32[128,4]{0,1:T(4,128)S(1)}, f32[128,4]{0,1:T(4,128)}, u32[]{:S(2)}) copy-start(f32[128,4]{0,1:T(4,128)} %param.6) | copy-start | bytes 6148
  31.4 1.6 %copy-start.4 = (f32[128]{0:T(128)S(1)}, f32[128]{0:T(128)}, u32[]{:S(2)}) copy-start(f32[128]{0:T(128)} %param.7) | copy-start | bytes 1540
Sparse Core Ops, SparseCore 0:
  33.1 98.8 all-gather.1
where the time goes:
time: 153 us
  waiting for transfers between devices  73.3 us (48%)
  blocking collectives  46.1 us (30%)
  local copies, waits for them, and re-layouts  15.1 us (10%)
  between operations  14.1 us (9%)
  other arithmetic  4.21 us (3%)
    all_gather x1, waiting for transfers between devices, shards(): serve_down = lax.all_gather(narrow_down, 'zero', axis=2, tiled=True)  73.3 us
    all_to_all x3, blocking collectives, copy_for_each(): return lax.all_to_all(copies, axis, split_axis=0, concat_axis=0, tiled=True)  46.1 us
    unnamed x11, local copies, waits for them, and re-layouts  14.2 us
  transfers between devices with their start and end apart: 1, of which 1 were waited for; matrix products, arithmetic and copies ran while one was open for 1% of the time, Pallas kernels for 0%

commit v1 on v0

v1 whole, which is shorter than its diff:
```python
import functools

import jax
import jax.numpy as jnp
from jax import lax
from jax.experimental import pallas as pl
from jax.experimental.pallas import tpu as pltpu
from jax.sharding import PartitionSpec as P


CORES = 2
LANES = 128
MiB = 2**20


def place_kernel(half, chips, plan, *refs):
    blocks, out_ref, sems = refs[: len(plan)], refs[-2], refs[-1]
    me = lax.axis_index("zero")
    core, chip = me % CORES, me // CORES
    sign = 1 - CORES * core
    copies = []
    for block, (step, e, across) in zip(blocks, plan):
        owner = core if not across else 1 - core
        source = (chip + (sign if across else -sign) * step + chips) % chips
        for side in range(CORES):
            column = pl.multiple_of((source * CORES + side) * LANES, LANES)
            here = block.at[side] if e is not None else None
            for n in ([e] if e is not None else range(half)):
                copies.append(
                    pltpu.make_async_copy(
                        here if e is not None else block.at[n, side],
                        out_ref.at[owner * half + n, :, pl.ds(column, LANES)],
                        sems.at[len(copies)],
                    )
                )
    for copy in copies:
        copy.start()
    for copy in copies:
        copy.wait()


def place(out, shape, half, chips, blocks):
    arrays = [b[0] for b in blocks]
    plan = tuple(b[1:] for b in blocks)
    count = sum(CORES * (1 if b[2] is not None else half) for b in blocks)
    any_spec = pl.BlockSpec(memory_space=pl.ANY)
    vmem = pl.BlockSpec(memory_space=pltpu.VMEM)
    size = sum(a.size * 2 for a in arrays)
    return pl.pallas_call(
        functools.partial(place_kernel, half, chips, plan),
        out_shape=jax.ShapeDtypeStruct(shape, jnp.bfloat16),
        in_specs=[vmem] * len(arrays) + ([] if out is None else [any_spec]),
        out_specs=any_spec,
        scratch_shapes=[pltpu.SemaphoreType.DMA((count,))],
        input_output_aliases={} if out is None else {len(arrays): 0},
        compiler_params=pltpu.CompilerParams(vmem_limit_bytes=size + MiB),
        cost_estimate=pl.CostEstimate(flops=0, bytes_accessed=2 * size, transcendentals=0),
    )(*arrays, *([] if out is None else [out]))


def shards(w_down, avg_down, router_weight, router_gain):
  experts, rows, cols = w_down.shape
  half = experts // CORES
  zero = lax.axis_size("zero")
  chips = zero // CORES
  me = lax.axis_index("zero")
  core = me % CORES
  partner = [(i, i ^ 1) for i in range(zero)]
  ring = [(i, (i + (CORES if i % CORES == 0 else -CORES)) % zero) for i in range(zero)]

  def fresh_of(first):
      w = lax.dynamic_slice_in_dim(w_down, first, half, 0)
      a = lax.dynamic_slice_in_dim(avg_down, first, half, 0)
      return w + a.astype(jnp.float32)

  theirs = fresh_of(half * (1 - core))
  other = lax.ppermute(theirs, "zero", partner)
  mine = fresh_of(half * core)

  fresh = w_down + avg_down.astype(jnp.float32)
  sums = jnp.sum(fresh * fresh, axis=2)
  lines = half * rows // 128
  sums = jnp.broadcast_to(sums.reshape(1, CORES, lines, 128), (chips, CORES, lines, 128)).reshape(zero, lines, 128)
  part = (router_weight * router_gain[:, None]).astype(jnp.bfloat16).astype(jnp.float32).T
  part = jnp.broadcast_to(part[None], (zero, *part.shape))
  met = lax.all_to_all(jnp.concatenate([sums, part], axis=1), "zero", split_axis=0, concat_axis=0, tiled=True)
  total = met[:, :lines].sum(axis=0).reshape(half, rows)
  scale = jnp.sqrt(total)
  columns = jnp.moveaxis(met[:, lines:], 0, 1).reshape(part.shape[1], -1).astype(jnp.bfloat16)

  own = (lax.broadcasted_iota(jnp.int32, (CORES, 1, 1), 0) == core)

  def chunk_of(e):
      fresh = jnp.where(own, mine[e][None], other[e][None])
      return (fresh / scale[e][None, :, None]).astype(jnp.bfloat16)

  shape = (experts, rows, cols * zero)
  put = functools.partial(place, shape=shape, half=half, chips=chips)
  out = None
  pending = []
  held = [chunk_of(e) for e in range(half)]
  for step in range(chips):
      following = []
      for e in range(half):
          if step < chips - 1:
              following.append(lax.ppermute(held[e], "zero", ring))
          blocks = [(held[e], step, e, False)]
          if step < chips - 1:
              if e == half - 1:
                  both = jnp.stack(held)
                  pending.append((lax.ppermute(both, "zero", partner), step, None, True))
              elif pending:
                  blocks.append(pending.pop())
          else:
              got = (lax.ppermute(held[e], "zero", partner), step, e, True)
              if pending:
                  blocks.append(pending.pop())
              pending.append(got)
          out = put(out, blocks=blocks)
      held = following
  out = put(out, blocks=pending)

  scale_other = lax.ppermute(scale, "zero", partner)
  scale_down = jnp.where(core == 0, jnp.concatenate([scale, scale_other]), jnp.concatenate([scale_other, scale]))

  bank = lax.axis_index("bank")
  n = lax.axis_size("bank")
  side = 4 if n == 16 else 1
  x, y = bank % side, bank // side

  def along(block, index, shift_of):
      gathered = jnp.zeros((side, *block.shape), block.dtype)
      gathered = lax.dynamic_update_slice_in_dim(gathered, block[None], index, 0)
      for k in range(1, side):
          got = lax.ppermute(block, "bank", [(b, shift_of(b, k)) for b in range(n)])
          gathered = lax.dynamic_update_slice_in_dim(gathered, got[None], (index - k) % side, 0)
      return gathered.reshape(side * block.shape[0], *block.shape[1:])

  columns = along(columns, x, lambda b, k: b // side * side + (b % side + k) % side)
  columns = along(columns, y, lambda b, k: (b + k * side) % n)
  return out, scale_down, columns.T


def solution(mesh):
    return jax.shard_map(
        shards,
        mesh=mesh,
        in_specs=(P("bank", None, "zero"), P("bank", None, "zero"), P("zero", "bank"), P("zero")),
        out_specs=(P("bank", None, None), P("bank", None), P()),
        check_vma=False,
    )
```

time: 153 us -> 148 us (0.967)
  starting transfers between devices: 0.04 us -> 47.5 us
  blocking collectives: 46.1 us -> 0 us
  Pallas kernels: 0 us -> 30.1 us
  waiting for transfers between devices: 73.3 us -> 46.1 us
  other arithmetic: 4.21 us -> 17.9 us
  between operations: 14.1 us -> 1.3 us
  local copies, waits for them, and re-layouts: 15.1 us -> 4 us
    all_gather x1 -> x0, waiting for transfers between devices: 73.3 us -> none  [shards(): serve_down = lax.all_gather(narrow_down, 'zero', axis=2, tiled=True)]
    all_to_all x3 -> x0, blocking collectives: 46.1 us -> none  [copy_for_each(): return lax.all_to_all(copies, axis, split_axis=0, concat_axis=0, tiled=True)]
    ppermute x0 -> x31, starting transfers between devices: none -> 40.6 us  [the longest x14 18.1 us: shards(): following.append(lax.ppermute(held[e], 'zero', ring))]
    ppermute x0 -> x31, waiting for transfers between devices: none -> 36 us  [the longest x14 36 us: shards(): following.append(lax.ppermute(held[e], 'zero', ring))]
    pallas_call x0 -> x17, Pallas kernels: none -> 30.1 us  [place(): pl.pallas_call(functools.partial(place_kernel, half, chips, plan), out_sh...]
    unnamed x11 -> x12, local copies, waits for them, and re-layouts: 14.2 us -> 2.42 us
    all_to_all x0 -> x1, waiting for transfers between devices: none -> 10 us  [shards(): lax.all_to_all(jnp.concatenate([sums, part], axis=1), 'zero', split_axis=...]
    another operation x0 -> x7, other arithmetic: none -> 9.27 us  [shards(): both = jnp.stack(held)]
  transfers between devices with their start and end apart: 1 -> 32, of which waited for: 1 -> 12; matrix products, arithmetic and copies ran while one was open for 1% -> 11% of each run, Pallas kernels for 0% -> 19%
where the time goes in v1:
time: 148 us; the launch traced here: 147 us
  starting transfers between devices  47.5 us (32%)
  waiting for transfers between devices  46.1 us (31%)
  Pallas kernels  30.1 us (20%)
  other arithmetic  17.9 us (12%)
  local copies, waits for them, and re-layouts  4 us (3%)
    ppermute x14, waiting for transfers between devices, shards(): following.append(lax.ppermute(held[e], 'zero', ring))  36 us
    pallas_call x17, Pallas kernels, place(): pl.pallas_call(functools.partial(place_kernel, half, chips, plan), out_sh...  30.1 us
    ppermute x14, starting transfers between devices, shards(): following.append(lax.ppermute(held[e], 'zero', ring))  18.1 us
    all_to_all x1, waiting for transfers between devices, shards(): lax.all_to_all(jnp.concatenate([sums, part], axis=1), 'zero', split_axis=...  10 us
    ppermute x6, starting transfers between devices, along(): got = lax.ppermute(block, 'bank', [(b, shift_of(b, k)) for b in range(n)])  9.88 us
    another operation x7, other arithmetic, shards(): both = jnp.stack(held)  9.27 us
    all_to_all x1, starting transfers between devices, shards(): lax.all_to_all(jnp.concatenate([sums, part], axis=1), 'zero', split_axis=...  6.88 us
    ppermute x7, starting transfers between devices, shards(): pending.append((lax.ppermute(both, 'zero', partner), step, None, True))  4.21 us
  transfers between devices with their start and end apart: 32, of which 12 were waited for; matrix products, arithmetic and copies ran while one was open for 11% of the time, Pallas kernels for 19%

profile of v1, /device:TPU:1, one launch (start us, length us, event | category | flops | bytes accessed | tf_op | source)
XLA Modules:
  0.0 146.9 jit_solution(7319188427713092929)
XLA Ops:
  0.7 2.0 %convert_add_fusion.1 = (f32[2,1024,128]{2,1,0:T(8,128)S(1)}, f32[2,1024,128]{2,1,0:T(8,128)S(1)}) fusion(f32[4,1024,128]{2,1,0:T(8,128)} %param.4, s32[]{:T(128)S(6)} %select_n.105, bf16[4,1024,128]{2,1,0:T(8,128)(2,1)} %param.5, s32[]{:T(128)S(6)} %select_n.106), kind=kLoop, calls=%fused_computation.13 | loop fusion | flops 1048576 | bytes 5242888 | tf_op jit(solution)/shard_map/add | solution.py:74
  2.7 3.3 %collective-permute-start = (f32[2,1024,128]{2,1,0:T(8,128)S(1)}, f32[2,1024,128]{2,1,0:T(8,128)}, u32[]{:S(2)}, u32[]{:S(2)}) collective-permute-start(f32[2,1024,128]{2,1,0:T(8,128)S(1)} %get-tuple-element.4), channel_id=1, source_target_pairs={{0,1},{1,0},{2,3},{3,2},{4,5},{5,4},{6,7},{7,6},{8,9},{9,8},{10,11... | collective-permute-start | bytes 3145736 | tf_op jit(solution)/shard_map/ppermute | solution.py:77
  6.0 2.5 %multiply_reduce_fusion = f32[4,1024]{1,0:T(4,128)S(1)} fusion(f32[4,1024,128]{2,1,0:T(8,128)} %param.4, bf16[4,1024,128]{2,1,0:T(8,128)(2,1)} %param.5), kind=kLoop, calls=%fused_computation | loop fusion | flops 2093056 | bytes 3162112 | tf_op jit(solution)/shard_map/reduce_sum | solution.py:81
  9.9 6.9 %all-to-all-start = ((f32[16,20,128]{2,1,0:T(8,128)}), f32[16,20,128]{2,1,0:T(8,128)S(1)}, u32[]{:S(2)}, u32[]{:S(2)}) async-start(f32[16,20,128]{2,1,0:T(8,128)} %pad_maximum_fusion.7), calls=%async_computation | async-start | bytes 393216 | tf_op jit(solution)/shard_map/all_to_all | solution.py:86
  16.9 10.0 %all-to-all-done = f32[16,20,128]{2,1,0:T(8,128)S(1)} async-done(((f32[16,20,128]{2,1,0:T(8,128)}), f32[16,20,128]{2,1,0:T(8,128)S(1)}, u32[]{:S(2)}, u32[]{:S(2)}) %all-to-all-start) | async-done | bytes 163872 | tf_op jit(solution)/shard_map/all_to_all | solution.py:86
  32.0 2.5 %collective-permute-start.26 = (bf16[4,2048]{1,0:T(4,128)(2,1)S(1)}, bf16[4,2048]{1,0:T(4,128)(2,1)S(1)}, u32[]{:S(2)}, u32[]{:S(2)}) collective-permute-start(bf16[4,2048]{1,0:T(4,128)(2,1)S(1)} %fusion), channel_id=1, source_target_pairs={{0,32},{16,48},{32,0},{48,16},{64,96},{80,112},{96,64},{112,80},{1... | collective-permute-start | bytes 49160 | tf_op jit(solution)/shard_map/ppermute | solution.py:135
  39.0 4.0 %collective-permute-done.1.refs_0_ = bf16[2,1024,128]{2,1,0:T(8,128)(2,1)S(1)} collective-permute-done((bf16[2,1024,128]{2,1,0:T(8,128)(2,1)S(1)}, bf16[2,1024,128]{2,1,0:T(8,128)(2,1)S(1)}, u32[]{:S(2)}, u32[]{:S(2)}) %collective-permute-start.1) | collective-permute-done | bytes 524320 | tf_op jit(solution)/shard_map/ppermute | solution.py:106
  45.7 3.0 %collective-permute-done.10.refs_0_ = bf16[2,1024,128]{2,1,0:T(8,128)(2,1)S(1)} collective-permute-done((bf16[2,1024,128]{2,1,0:T(8,128)(2,1)S(1)}, bf16[2,1024,128]{2,1,0:T(8,128)(2,1)S(1)}, u32[]{:S(2)}, u32[]{:S(2)}) %collective-permute-start.10) | collective-permute-done | bytes 524320 | tf_op jit(solution)/shard_map/ppermute | solution.py:106
  49.6 4.7 %collective-permute-done.2.refs_0_ = bf16[2,1024,128]{2,1,0:T(8,128)(2,1)S(1)} collective-permute-done((bf16[2,1024,128]{2,1,0:T(8,128)(2,1)S(1)}, bf16[2,1024,128]{2,1,0:T(8,128)(2,1)S(1)}, u32[]{:S(2)}, u32[]{:S(2)}) %collective-permute-start.2) | collective-permute-done | bytes 524320 | tf_op jit(solution)/shard_map/ppermute | solution.py:106
  57.2 2.7 %collective-permute-done.11.refs_0_ = bf16[2,1024,128]{2,1,0:T(8,128)(2,1)S(1)} collective-permute-done((bf16[2,1024,128]{2,1,0:T(8,128)(2,1)S(1)}, bf16[2,1024,128]{2,1,0:T(8,128)(2,1)S(1)}, u32[]{:S(2)}, u32[]{:S(2)}) %collective-permute-start.11) | collective-permute-done | bytes 524320 | tf_op jit(solution)/shard_map/ppermute | solution.py:106
  60.8 4.8 %collective-permute-done.3.refs_0_ = bf16[2,1024,128]{2,1,0:T(8,128)(2,1)} collective-permute-done((bf16[2,1024,128]{2,1,0:T(8,128)(2,1)S(1)}, bf16[2,1024,128]{2,1,0:T(8,128)(2,1)}, u32[]{:S(2)}, u32[]{:S(2)}) %collective-permute-start.3) | collective-permute-done | bytes 524320 | tf_op jit(solution)/shard_map/ppermute | solution.py:106
  69.0 2.2 %collective-permute-done.12.refs_0_ = bf16[2,1024,128]{2,1,0:T(8,128)(2,1)} collective-permute-done((bf16[2,1024,128]{2,1,0:T(8,128)(2,1)S(1)}, bf16[2,1024,128]{2,1,0:T(8,128)(2,1)}, u32[]{:S(2)}, u32[]{:S(2)}) %collective-permute-start.12) | collective-permute-done | bytes 524320 | tf_op jit(solution)/shard_map/ppermute | solution.py:106
  72.1 4.7 %collective-permute-done.4.refs_0_ = bf16[2,1024,128]{2,1,0:T(8,128)(2,1)} collective-permute-done((bf16[2,1024,128]{2,1,0:T(8,128)(2,1)}, bf16[2,1024,128]{2,1,0:T(8,128)(2,1)}, u32[]{:S(2)}, u32[]{:S(2)}) %collective-permute-start.4) | collective-permute-done | bytes 524320 | tf_op jit(solution)/shard_map/ppermute | solution.py:106
  78.8 2.9 %collective-permute-start.29 = (bf16[16,2048]{1,0:T(8,128)(2,1)S(1)}, bf16[16,2048]{1,0:T(8,128)(2,1)S(1)}, u32[]{:S(2)}, u32[]{:S(2)}) collective-permute-start(bf16[16,2048]{1,0:T(8,128)(2,1)S(1)} %reshape.64), channel_id=1, source_target_pairs={{0,128},{16,144},{32,160},{48,176},{64,192},{80,208},{96,224},{112... | collective-permute-start | bytes 196616 | tf_op jit(solution)/shard_map/ppermute | solution.py:135
  82.5 2.1 %pad_maximum_fusion.3 = bf16[2,2,1024,128]{3,2,1,0:T(8,128)(2,1)} fusion(bf16[1,2,1024,128]{3,2,1,0:T(8,128)(2,1)} %bitcast.15, bf16[1,2,1024,128]{3,2,1,0:T(8,128)(2,1)S(1)} %bitcast.53), kind=kLoop, calls=%fused_computation.4 | loop fusion | flops 524288 | bytes 2097152 | tf_op jit(solution)/shard_map/stack | solution.py:110
  87.3 3.0 %collective-permute-start.14 = (bf16[2,1024,128]{2,1,0:T(8,128)(2,1)}, bf16[2,1024,128]{2,1,0:T(8,128)(2,1)}, u32[]{:S(2)}, u32[]{:S(2)}) collective-permute-start(bf16[2,1024,128]{2,1,0:T(8,128)(2,1)} %collective-permute-done.13.refs_0_), channel_id=1, source_target_pairs={{0,2},{1,15},{2,4},{3,1},{4,6},{5,3},{6,8},{7,5},{8,10},{9,7},{10,... | collective-permute-start | bytes 1572872 | tf_op jit(solution)/shard_map/ppermute | solution.py:106
  93.7 3.0 %collective-permute-done.14.refs_0_ = bf16[2,1024,128]{2,1,0:T(8,128)(2,1)} collective-permute-done((bf16[2,1024,128]{2,1,0:T(8,128)(2,1)}, bf16[2,1024,128]{2,1,0:T(8,128)(2,1)}, u32[]{:S(2)}, u32[]{:S(2)}) %collective-permute-start.14) | collective-permute-done | bytes 524320 | tf_op jit(solution)/shard_map/ppermute | solution.py:106
  96.7 3.1 %collective-permute-start.15 = (bf16[2,1024,128]{2,1,0:T(8,128)(2,1)}, bf16[2,1024,128]{2,1,0:T(8,128)(2,1)S(1)}, u32[]{:S(2)}, u32[]{:S(2)}) collective-permute-start(bf16[2,1024,128]{2,1,0:T(8,128)(2,1)} %collective-permute-done.14.refs_0_), channel_id=1, source_target_pairs={{0,2},{1,15},{2,4},{3,1},{4,6},{5,3},{6,8},{7,5},{8,10},{9,7},{10,... | collective-permute-start | bytes 1572872 | tf_op jit(solution)/shard_map/ppermute | solution.py:106
  99.8 2.5 %collective-permute-done.6.refs_0_ = bf16[2,1024,128]{2,1,0:T(8,128)(2,1)} collective-permute-done((bf16[2,1024,128]{2,1,0:T(8,128)(2,1)}, bf16[2,1024,128]{2,1,0:T(8,128)(2,1)}, u32[]{:S(2)}, u32[]{:S(2)}) %collective-permute-start.6) | collective-permute-done | bytes 524320 | tf_op jit(solution)/shard_map/ppermute | solution.py:106
  102.3 3.1 %collective-permute-start.7 = (bf16[2,1024,128]{2,1,0:T(8,128)(2,1)}, bf16[2,1024,128]{2,1,0:T(8,128)(2,1)}, u32[]{:S(2)}, u32[]{:S(2)}) collective-permute-start(bf16[2,1024,128]{2,1,0:T(8,128)(2,1)} %collective-permute-done.6.refs_0_), channel_id=1, source_target_pairs={{0,2},{1,15},{2,4},{3,1},{4,6},{5,3},{6,8},{7,5},{8,10},{9,7},{10,... | collective-permute-start | bytes 1572872 | tf_op jit(solution)/shard_map/ppermute | solution.py:106
  109.6 4.0 %collective-permute-done.7.refs_0_ = bf16[2,1024,128]{2,1,0:T(8,128)(2,1)} collective-permute-done((bf16[2,1024,128]{2,1,0:T(8,128)(2,1)}, bf16[2,1024,128]{2,1,0:T(8,128)(2,1)}, u32[]{:S(2)}, u32[]{:S(2)}) %collective-permute-start.7) | collective-permute-done | bytes 524320 | tf_op jit(solution)/shard_map/ppermute | solution.py:106
  118.1 2.4 %shard_map.69.refs_1_ = bf16[4,1024,2048]{2,1,0:T(8,128)(2,1)} custom-call(bf16[2,1024,128]{2,1,0:T(8,128)(2,1)S(1)} %collective-permute-done.9.refs_0_, bf16[2,2,1024,128]{3,2,1,0:T(8,128)(2,1)} %collective-permute-done.23.refs_1_, bf16[4,1024,2048]{2,1,0:T(8,128)(2,1)} %shard_map.68.refs_2_), custom_call_target="tpu_custom_call", output_to_operand_aliasing={{}: (2, {})} | custom-call | bytes 3145728 | tf_op jit(solution)/shard_map/pallas_call | solution.py:49
  121.4 2.4 %shard_map.71.refs_1_ = bf16[4,1024,2048]{2,1,0:T(8,128)(2,1)} custom-call(bf16[2,1024,128]{2,1,0:T(8,128)(2,1)S(1)} %collective-permute-done.10.refs_0_, bf16[2,2,1024,128]{3,2,1,0:T(8,128)(2,1)} %collective-permute-done.22.refs_1_, bf16[4,1024,2048]{2,1,0:T(8,128)(2,1)} %shard_map.70.refs_2_), custom_call_target="tpu_custom_call", output_to_operand_aliasing={{}: (2, {})} | custom-call | bytes 3145728 | tf_op jit(solution)/shard_map/pallas_call | solution.py:49
  124.6 2.4 %shard_map.73.refs_1_ = bf16[4,1024,2048]{2,1,0:T(8,128)(2,1)} custom-call(bf16[2,1024,128]{2,1,0:T(8,128)(2,1)S(1)} %collective-permute-done.11.refs_0_, bf16[2,2,1024,128]{3,2,1,0:T(8,128)(2,1)} %collective-permute-done.21.refs_1_, bf16[4,1024,2048]{2,1,0:T(8,128)(2,1)} %shard_map.72.refs_2_), custom_call_target="tpu_custom_call", output_to_operand_aliasing={{}: (2, {})} | custom-call | bytes 3145728 | tf_op jit(solution)/shard_map/pallas_call | solution.py:49
  127.0 1.9 %shard_map.74.refs_2_ = bf16[4,1024,2048]{2,1,0:T(8,128)(2,1)} custom-call(bf16[2,1024,128]{2,1,0:T(8,128)(2,1)} %collective-permute-done.3.refs_0_, bf16[4,1024,2048]{2,1,0:T(8,128)(2,1)} %shard_map.73.refs_1_), custom_call_target="tpu_custom_call", output_to_operand_aliasing={{}: (1, {})} | custom-call | bytes 1048576 | tf_op jit(solution)/shard_map/pallas_call | solution.py:49
  128.9 2.6 %shard_map.75.refs_1_ = bf16[4,1024,2048]{2,1,0:T(8,128)(2,1)} custom-call(bf16[2,1024,128]{2,1,0:T(8,128)(2,1)} %collective-permute-done.12.refs_0_, bf16[2,2,1024,128]{3,2,1,0:T(8,128)(2,1)} %collective-permute-done.20.refs_1_, bf16[4,1024,2048]{2,1,0:T(8,128)(2,1)} %shard_map.74.refs_2_), custom_call_target="tpu_custom_call", output_to_operand_aliasing={{}: (2, {})} | custom-call | bytes 3145728 | tf_op jit(solution)/shard_map/pallas_call | solution.py:49
  131.5 1.9 %shard_map.76.refs_2_ = bf16[4,1024,2048]{2,1,0:T(8,128)(2,1)} custom-call(bf16[2,1024,128]{2,1,0:T(8,128)(2,1)} %collective-permute-done.4.refs_0_, bf16[4,1024,2048]{2,1,0:T(8,128)(2,1)} %shard_map.75.refs_1_), custom_call_target="tpu_custom_call", output_to_operand_aliasing={{}: (1, {})} | custom-call | bytes 1048576 | tf_op jit(solution)/shard_map/pallas_call | solution.py:49
  133.3 2.2 %shard_map.77.refs_1_ = bf16[4,1024,2048]{2,1,0:T(8,128)(2,1)} custom-call(bf16[2,1024,128]{2,1,0:T(8,128)(2,1)} %collective-permute-done.13.refs_0_, bf16[2,2,1024,128]{3,2,1,0:T(8,128)(2,1)S(1)} %collective-permute-done.19.refs_1_, bf16[4,1024,2048]{2,1,0:T(8,128)(2,1)} %shard_map.76.refs_2_), custom_call_target="tpu_custom_call", output_to_operand_aliasing={{}: (2, {})} | custom-call | bytes 3145728 | tf_op jit(solution)/shard_map/pallas_call | solution.py:49
  135.6 1.9 %shard_map.78.refs_2_ = bf16[4,1024,2048]{2,1,0:T(8,128)(2,1)} custom-call(bf16[2,1024,128]{2,1,0:T(8,128)(2,1)} %collective-permute-done.5.refs_0_, bf16[4,1024,2048]{2,1,0:T(8,128)(2,1)} %shard_map.77.refs_1_), custom_call_target="tpu_custom_call", output_to_operand_aliasing={{}: (1, {})} | custom-call | bytes 1048576 | tf_op jit(solution)/shard_map/pallas_call | solution.py:49
  137.4 2.2 %shard_map.79.refs_1_ = bf16[4,1024,2048]{2,1,0:T(8,128)(2,1)} custom-call(bf16[2,1024,128]{2,1,0:T(8,128)(2,1)} %collective-permute-done.14.refs_0_, bf16[2,2,1024,128]{3,2,1,0:T(8,128)(2,1)S(1)} %collective-permute-done.18.refs_1_, bf16[4,1024,2048]{2,1,0:T(8,128)(2,1)} %shard_map.78.refs_2_), custom_call_target="tpu_custom_call", output_to_operand_aliasing={{}: (2, {})} | custom-call | bytes 3145728 | tf_op jit(solution)/shard_map/pallas_call | solution.py:49
  139.7 1.9 %shard_map.80.refs_2_ = bf16[4,1024,2048]{2,1,0:T(8,128)(2,1)} custom-call(bf16[2,1024,128]{2,1,0:T(8,128)(2,1)} %collective-permute-done.6.refs_0_, bf16[4,1024,2048]{2,1,0:T(8,128)(2,1)} %shard_map.79.refs_1_), custom_call_target="tpu_custom_call", output_to_operand_aliasing={{}: (1, {})} | custom-call | bytes 1048576 | tf_op jit(solution)/shard_map/pallas_call | solution.py:49
  142.8 2.0 %shard_map.82.refs_1_ = bf16[4,1024,2048]{2,1,0:T(8,128)(2,1)} custom-call(bf16[2,1024,128]{2,1,0:T(8,128)(2,1)} %collective-permute-done.7.refs_0_, bf16[2,1024,128]{2,1,0:T(8,128)(2,1)S(1)} %collective-permute-done.16.refs_1_, bf16[4,1024,2048]{2,1,0:T(8,128)(2,1)} %shard_map.81.refs_2_), custom_call_target="tpu_custom_call", output_to_operand_aliasing={{}: (2, {})} | custom-call | bytes 2097152 | tf_op jit(solution)/shard_map/pallas_call | solution.py:49
  (98 shorter events, 44.9 us)
Async XLA Ops:
  2.7 24.3 %collective-permute-start = (f32[2,1024,128]{2,1,0:T(8,128)S(1)}, f32[2,1024,128]{2,1,0:T(8,128)}, u32[]{:S(2)}, u32[]{:S(2)}) collective-permute-start(f32[2,1024,128]{2,1,0:T(8,128)S(1)} %get-tuple-element.4), channel_id=1, source_target_pairs={{0,1},{1,0},{2,3},{3,2},{4,5},{5,4},{6,7},{7,6},{8,9},{9,8},{10,11... | collective-permute-start | bytes 3145736 | tf_op jit(solution)/shard_map/ppermute | solution.py:77
  9.9 17.1 %all-to-all-start = ((f32[16,20,128]{2,1,0:T(8,128)}), f32[16,20,128]{2,1,0:T(8,128)S(1)}, u32[]{:S(2)}, u32[]{:S(2)}) async-start(f32[16,20,128]{2,1,0:T(8,128)} %pad_maximum_fusion.7), calls=%async_computation | async-start | bytes 393216 | tf_op jit(solution)/shard_map/all_to_all | solution.py:86
  29.1 8.3 %collective-permute-start.9 = (bf16[2,1024,128]{2,1,0:T(8,128)(2,1)S(1)}, bf16[2,1024,128]{2,1,0:T(8,128)(2,1)S(1)}, u32[]{:S(2)}, u32[]{:S(2)}) collective-permute-start(bf16[2,1024,128]{2,1,0:T(8,128)(2,1)S(1)} %get-tuple-element.13.refs_0_), channel_id=1, source_target_pairs={{0,2},{1,15},{2,4},{3,1},{4,6},{5,3},{6,8},{7,5},{8,10},{9,7},{10,... | collective-permute-start | bytes 1572872 | tf_op jit(solution)/shard_map/ppermute | solution.py:106
  30.1 12.9 %collective-permute-start.1 = (bf16[2,1024,128]{2,1,0:T(8,128)(2,1)S(1)}, bf16[2,1024,128]{2,1,0:T(8,128)(2,1)S(1)}, u32[]{:S(2)}, u32[]{:S(2)}) collective-permute-start(bf16[2,1024,128]{2,1,0:T(8,128)(2,1)S(1)} %get-tuple-element.14.refs_0_), channel_id=1, source_target_pairs={{0,2},{1,15},{2,4},{3,1},{4,6},{5,3},{6,8},{7,5},{8,10},{9,7},{10,... | collective-permute-start | bytes 1572872 | tf_op jit(solution)/shard_map/ppermute | solution.py:106
  30.8 4.9 %collective-permute-start.25 = (bf16[4,2048]{1,0:T(4,128)(2,1)S(1)}, bf16[4,2048]{1,0:T(4,128)(2,1)S(1)}, u32[]{:S(2)}, u32[]{:S(2)}) collective-permute-start(bf16[4,2048]{1,0:T(4,128)(2,1)S(1)} %fusion), channel_id=1, source_target_pairs={{0,16},{16,32},{32,48},{48,0},{64,80},{80,96},{96,112},{112,64},{1... | collective-permute-start | bytes 49160 | tf_op jit(solution)/shard_map/ppermute | solution.py:135
  32.0 24.3 %collective-permute-start.26 = (bf16[4,2048]{1,0:T(4,128)(2,1)S(1)}, bf16[4,2048]{1,0:T(4,128)(2,1)S(1)}, u32[]{:S(2)}, u32[]{:S(2)}) collective-permute-start(bf16[4,2048]{1,0:T(4,128)(2,1)S(1)} %fusion), channel_id=1, source_target_pairs={{0,32},{16,48},{32,0},{48,16},{64,96},{80,112},{96,64},{112,80},{1... | collective-permute-start | bytes 49160 | tf_op jit(solution)/shard_map/ppermute | solution.py:135
  34.4 32.1 %collective-permute-start.27 = (bf16[4,2048]{1,0:T(4,128)(2,1)S(1)}, bf16[4,2048]{1,0:T(4,128)(2,1)S(1)}, u32[]{:S(2)}, u32[]{:S(2)}) collective-permute-start(bf16[4,2048]{1,0:T(4,128)(2,1)S(1)} %fusion), channel_id=1, source_target_pairs={{0,48},{16,0},{32,16},{48,32},{64,112},{80,64},{96,80},{112,96},{1... | collective-permute-start | bytes 49160 | tf_op jit(solution)/shard_map/ppermute | solution.py:135
  35.7 43.2 %collective-permute-start.24 = (f32[2,1024]{1,0:T(2,128)S(1)}, f32[2,1024]{1,0:T(2,128)S(1)}, u32[]{:S(2)}, u32[]{:S(2)}) collective-permute-start(f32[2,1024]{1,0:T(2,128)S(1)} %sqrt.7), channel_id=1, source_target_pairs={{0,1},{1,0},{2,3},{3,2},{4,5},{5,4},{6,7},{7,6},{8,9},{9,8},{10,11... | collective-permute-start | bytes 24584 | tf_op jit(solution)/shard_map/ppermute | solution.py:123
  37.4 11.2 %collective-permute-start.10 = (bf16[2,1024,128]{2,1,0:T(8,128)(2,1)S(1)}, bf16[2,1024,128]{2,1,0:T(8,128)(2,1)S(1)}, u32[]{:S(2)}, u32[]{:S(2)}) collective-permute-start(bf16[2,1024,128]{2,1,0:T(8,128)(2,1)S(1)} %collective-permute-done.9.refs_0_), channel_id=1, source_target_pairs={{0,2},{1,15},{2,4},{3,1},{4,6},{5,3},{6,8},{7,5},{8,10},{9,7},{10,... | collective-permute-start | bytes 1572872 | tf_op jit(solution)/shard_map/ppermute | solution.py:106
  43.0 11.2 %collective-permute-start.2 = (bf16[2,1024,128]{2,1,0:T(8,128)(2,1)S(1)}, bf16[2,1024,128]{2,1,0:T(8,128)(2,1)S(1)}, u32[]{:S(2)}, u32[]{:S(2)}) collective-permute-start(bf16[2,1024,128]{2,1,0:T(8,128)(2,1)S(1)} %collective-permute-done.1.refs_0_), channel_id=1, source_target_pairs={{0,2},{1,15},{2,4},{3,1},{4,6},{5,3},{6,8},{7,5},{8,10},{9,7},{10,... | collective-permute-start | bytes 1572872 | tf_op jit(solution)/shard_map/ppermute | solution.py:106
  48.6 11.2 %collective-permute-start.11 = (bf16[2,1024,128]{2,1,0:T(8,128)(2,1)S(1)}, bf16[2,1024,128]{2,1,0:T(8,128)(2,1)S(1)}, u32[]{:S(2)}, u32[]{:S(2)}) collective-permute-start(bf16[2,1024,128]{2,1,0:T(8,128)(2,1)S(1)} %collective-permute-done.10.refs_0_), channel_id=1, source_target_pairs={{0,2},{1,15},{2,4},{3,1},{4,6},{5,3},{6,8},{7,5},{8,10},{9,7},{10,... | collective-permute-start | bytes 1572872 | tf_op jit(solution)/shard_map/ppermute | solution.py:106
  54.3 11.3 %collective-permute-start.3 = (bf16[2,1024,128]{2,1,0:T(8,128)(2,1)S(1)}, bf16[2,1024,128]{2,1,0:T(8,128)(2,1)}, u32[]{:S(2)}, u32[]{:S(2)}) collective-permute-start(bf16[2,1024,128]{2,1,0:T(8,128)(2,1)S(1)} %collective-permute-done.2.refs_0_), channel_id=1, source_target_pairs={{0,2},{1,15},{2,4},{3,1},{4,6},{5,3},{6,8},{7,5},{8,10},{9,7},{10,... | collective-permute-start | bytes 1572872 | tf_op jit(solution)/shard_map/ppermute | solution.py:106
  56.2 31.0 %collective-permute-start.23 = (bf16[2,2,1024,128]{3,2,1,0:T(8,128)(2,1)}, bf16[2,2,1024,128]{3,2,1,0:T(8,128)(2,1)}, u32[]{:S(2)}, u32[]{:S(2)}) collective-permute-start(bf16[2,2,1024,128]{3,2,1,0:T(8,128)(2,1)} %pad_maximum_fusion.6), channel_id=1, source_target_pairs={{0,1},{1,0},{2,3},{3,2},{4,5},{5,4},{6,7},{7,6},{8,9},{9,8},{10,11... | collective-permute-start | bytes 3145736 | tf_op jit(solution)/shard_map/ppermute | solution.py:111
  59.9 11.3 %collective-permute-start.12 = (bf16[2,1024,128]{2,1,0:T(8,128)(2,1)S(1)}, bf16[2,1024,128]{2,1,0:T(8,128)(2,1)}, u32[]{:S(2)}, u32[]{:S(2)}) collective-permute-start(bf16[2,1024,128]{2,1,0:T(8,128)(2,1)S(1)} %collective-permute-done.11.refs_0_), channel_id=1, source_target_pairs={{0,2},{1,15},{2,4},{3,1},{4,6},{5,3},{6,8},{7,5},{8,10},{9,7},{10,... | collective-permute-start | bytes 1572872 | tf_op jit(solution)/shard_map/ppermute | solution.py:106
  65.6 11.2 %collective-permute-start.4 = (bf16[2,1024,128]{2,1,0:T(8,128)(2,1)}, bf16[2,1024,128]{2,1,0:T(8,128)(2,1)}, u32[]{:S(2)}, u32[]{:S(2)}) collective-permute-start(bf16[2,1024,128]{2,1,0:T(8,128)(2,1)} %collective-permute-done.3.refs_0_), channel_id=1, source_target_pairs={{0,2},{1,15},{2,4},{3,1},{4,6},{5,3},{6,8},{7,5},{8,10},{9,7},{10,... | collective-permute-start | bytes 1572872 | tf_op jit(solution)/shard_map/ppermute | solution.py:106
  66.6 15.2 %collective-permute-start.28 = (bf16[16,2048]{1,0:T(8,128)(2,1)S(1)}, bf16[16,2048]{1,0:T(8,128)(2,1)S(1)}, u32[]{:S(2)}, u32[]{:S(2)}) collective-permute-start(bf16[16,2048]{1,0:T(8,128)(2,1)S(1)} %reshape.64), channel_id=1, source_target_pairs={{0,64},{16,80},{32,96},{48,112},{64,128},{80,144},{96,160},{112,17... | collective-permute-start | bytes 196616 | tf_op jit(solution)/shard_map/ppermute | solution.py:135
  71.2 16.0 %collective-permute-start.13 = (bf16[2,1024,128]{2,1,0:T(8,128)(2,1)}, bf16[2,1024,128]{2,1,0:T(8,128)(2,1)}, u32[]{:S(2)}, u32[]{:S(2)}) collective-permute-start(bf16[2,1024,128]{2,1,0:T(8,128)(2,1)} %collective-permute-done.12.refs_0_), channel_id=1, source_target_pairs={{0,2},{1,15},{2,4},{3,1},{4,6},{5,3},{6,8},{7,5},{8,10},{9,7},{10,... | collective-permute-start | bytes 1572872 | tf_op jit(solution)/shard_map/ppermute | solution.py:106
  76.8 13.5 %collective-permute-start.5 = (bf16[2,1024,128]{2,1,0:T(8,128)(2,1)}, bf16[2,1024,128]{2,1,0:T(8,128)(2,1)}, u32[]{:S(2)}, u32[]{:S(2)}) collective-permute-start(bf16[2,1024,128]{2,1,0:T(8,128)(2,1)} %collective-permute-done.4.refs_0_), channel_id=1, source_target_pairs={{0,2},{1,15},{2,4},{3,1},{4,6},{5,3},{6,8},{7,5},{8,10},{9,7},{10,... | collective-permute-start | bytes 1572872 | tf_op jit(solution)/shard_map/ppermute | solution.py:106
  78.8 5.8 %collective-permute-start.29 = (bf16[16,2048]{1,0:T(8,128)(2,1)S(1)}, bf16[16,2048]{1,0:T(8,128)(2,1)S(1)}, u32[]{:S(2)}, u32[]{:S(2)}) collective-permute-start(bf16[16,2048]{1,0:T(8,128)(2,1)S(1)} %reshape.64), channel_id=1, source_target_pairs={{0,128},{16,144},{32,160},{48,176},{64,192},{80,208},{96,224},{112... | collective-permute-start | bytes 196616 | tf_op jit(solution)/shard_map/ppermute | solution.py:135
  81.8 4.4 %collective-permute-start.30 = (bf16[16,2048]{1,0:T(8,128)(2,1)S(1)}, bf16[16,2048]{1,0:T(8,128)(2,1)S(1)}, u32[]{:S(2)}, u32[]{:S(2)}) collective-permute-start(bf16[16,2048]{1,0:T(8,128)(2,1)S(1)} %reshape.64), channel_id=1, source_target_pairs={{0,192},{16,208},{32,224},{48,240},{64,0},{80,16},{96,32},{112,48}... | collective-permute-start | bytes 196616 | tf_op jit(solution)/shard_map/ppermute | solution.py:135
  84.7 22.1 %collective-permute-start.22 = (bf16[2,2,1024,128]{3,2,1,0:T(8,128)(2,1)}, bf16[2,2,1024,128]{3,2,1,0:T(8,128)(2,1)}, u32[]{:S(2)}, u32[]{:S(2)}) collective-permute-start(bf16[2,2,1024,128]{3,2,1,0:T(8,128)(2,1)} %pad_maximum_fusion.5), channel_id=1, source_target_pairs={{0,1},{1,0},{2,3},{3,2},{4,5},{5,4},{6,7},{7,6},{8,9},{9,8},{10,11... | collective-permute-start | bytes 3145736 | tf_op jit(solution)/shard_map/ppermute | solution.py:111
  86.1 20.7 %collective-permute-start.21 = (bf16[2,2,1024,128]{3,2,1,0:T(8,128)(2,1)}, bf16[2,2,1024,128]{3,2,1,0:T(8,128)(2,1)}, u32[]{:S(2)}, u32[]{:S(2)}) collective-permute-start(bf16[2,2,1024,128]{3,2,1,0:T(8,128)(2,1)} %pad_maximum_fusion.4), channel_id=1, source_target_pairs={{0,1},{1,0},{2,3},{3,2},{4,5},{5,4},{6,7},{7,6},{8,9},{9,8},{10,11... | collective-permute-start | bytes 3145736 | tf_op jit(solution)/shard_map/ppermute | solution.py:111
  87.2 20.1 %collective-permute-start.20 = (bf16[2,2,1024,128]{3,2,1,0:T(8,128)(2,1)}, bf16[2,2,1024,128]{3,2,1,0:T(8,128)(2,1)}, u32[]{:S(2)}, u32[]{:S(2)}) collective-permute-start(bf16[2,2,1024,128]{3,2,1,0:T(8,128)(2,1)} %pad_maximum_fusion.3), channel_id=1, source_target_pairs={{0,1},{1,0},{2,3},{3,2},{4,5},{5,4},{6,7},{7,6},{8,9},{9,8},{10,11... | collective-permute-start | bytes 3145736 | tf_op jit(solution)/shard_map/ppermute | solution.py:111
  87.3 9.5 %collective-permute-start.14 = (bf16[2,1024,128]{2,1,0:T(8,128)(2,1)}, bf16[2,1024,128]{2,1,0:T(8,128)(2,1)}, u32[]{:S(2)}, u32[]{:S(2)}) collective-permute-start(bf16[2,1024,128]{2,1,0:T(8,128)(2,1)} %collective-permute-done.13.refs_0_), channel_id=1, source_target_pairs={{0,2},{1,15},{2,4},{3,1},{4,6},{5,3},{6,8},{7,5},{8,10},{9,7},{10,... | collective-permute-start | bytes 1572872 | tf_op jit(solution)/shard_map/ppermute | solution.py:106
  90.3 12.1 %collective-permute-start.6 = (bf16[2,1024,128]{2,1,0:T(8,128)(2,1)}, bf16[2,1024,128]{2,1,0:T(8,128)(2,1)}, u32[]{:S(2)}, u32[]{:S(2)}) collective-permute-start(bf16[2,1024,128]{2,1,0:T(8,128)(2,1)} %collective-permute-done.5.refs_0_), channel_id=1, source_target_pairs={{0,2},{1,15},{2,4},{3,1},{4,6},{5,3},{6,8},{7,5},{8,10},{9,7},{10,... | collective-permute-start | bytes 1572872 | tf_op jit(solution)/shard_map/ppermute | solution.py:106
  96.7 11.2 %collective-permute-start.15 = (bf16[2,1024,128]{2,1,0:T(8,128)(2,1)}, bf16[2,1024,128]{2,1,0:T(8,128)(2,1)S(1)}, u32[]{:S(2)}, u32[]{:S(2)}) collective-permute-start(bf16[2,1024,128]{2,1,0:T(8,128)(2,1)} %collective-permute-done.14.refs_0_), channel_id=1, source_target_pairs={{0,2},{1,15},{2,4},{3,1},{4,6},{5,3},{6,8},{7,5},{8,10},{9,7},{10,... | collective-permute-start | bytes 1572872 | tf_op jit(solution)/shard_map/ppermute | solution.py:106
  102.3 11.2 %collective-permute-start.7 = (bf16[2,1024,128]{2,1,0:T(8,128)(2,1)}, bf16[2,1024,128]{2,1,0:T(8,128)(2,1)}, u32[]{:S(2)}, u32[]{:S(2)}) collective-permute-start(bf16[2,1024,128]{2,1,0:T(8,128)(2,1)} %collective-permute-done.6.refs_0_), channel_id=1, source_target_pairs={{0,2},{1,15},{2,4},{3,1},{4,6},{5,3},{6,8},{7,5},{8,10},{9,7},{10,... | collective-permute-start | bytes 1572872 | tf_op jit(solution)/shard_map/ppermute | solution.py:106
  106.8 26.6 %collective-permute-start.19 = (bf16[2,2,1024,128]{3,2,1,0:T(8,128)(2,1)S(1)}, bf16[2,2,1024,128]{3,2,1,0:T(8,128)(2,1)S(1)}, u32[]{:S(2)}, u32[]{:S(2)}) collective-permute-start(bf16[2,2,1024,128]{3,2,1,0:T(8,128)(2,1)S(1)} %pad_maximum_fusion.2), channel_id=1, source_target_pairs={{0,1},{1,0},{2,3},{3,2},{4,5},{5,4},{6,7},{7,6},{8,9},{9,8},{10,11... | collective-permute-start | bytes 3145736 | tf_op jit(solution)/shard_map/ppermute | solution.py:111
  106.9 30.6 %collective-permute-start.18 = (bf16[2,2,1024,128]{3,2,1,0:T(8,128)(2,1)S(1)}, bf16[2,2,1024,128]{3,2,1,0:T(8,128)(2,1)S(1)}, u32[]{:S(2)}, u32[]{:S(2)}) collective-permute-start(bf16[2,2,1024,128]{3,2,1,0:T(8,128)(2,1)S(1)} %pad_maximum_fusion.1), channel_id=1, source_target_pairs={{0,1},{1,0},{2,3},{3,2},{4,5},{5,4},{6,7},{7,6},{8,9},{9,8},{10,11... | collective-permute-start | bytes 3145736 | tf_op jit(solution)/shard_map/ppermute | solution.py:111
  107.4 34.2 %collective-permute-start.17 = (bf16[2,2,1024,128]{3,2,1,0:T(8,128)(2,1)S(1)}, bf16[2,2,1024,128]{3,2,1,0:T(8,128)(2,1)S(1)}, u32[]{:S(2)}, u32[]{:S(2)}) collective-permute-start(bf16[2,2,1024,128]{3,2,1,0:T(8,128)(2,1)S(1)} %pad_maximum_fusion), channel_id=1, source_target_pairs={{0,1},{1,0},{2,3},{3,2},{4,5},{5,4},{6,7},{7,6},{8,9},{9,8},{10,11... | collective-permute-start | bytes 3145736 | tf_op jit(solution)/shard_map/ppermute | solution.py:111
  108.0 34.8 %collective-permute-start.16 = (bf16[2,1024,128]{2,1,0:T(8,128)(2,1)S(1)}, bf16[2,1024,128]{2,1,0:T(8,128)(2,1)S(1)}, u32[]{:S(2)}, u32[]{:S(2)}) collective-permute-start(bf16[2,1024,128]{2,1,0:T(8,128)(2,1)S(1)} %collective-permute-done.15.refs_0_), channel_id=1, source_target_pairs={{0,1},{1,0},{2,3},{3,2},{4,5},{5,4},{6,7},{7,6},{8,9},{9,8},{10,11... | collective-permute-start | bytes 1572872 | tf_op jit(solution)/shard_map/ppermute | solution.py:115
  113.6 31.3 %collective-permute-start.8 = (bf16[2,1024,128]{2,1,0:T(8,128)(2,1)}, bf16[2,1024,128]{2,1,0:T(8,128)(2,1)}, u32[]{:S(2)}, u32[]{:S(2)}) collective-permute-start(bf16[2,1024,128]{2,1,0:T(8,128)(2,1)} %collective-permute-done.7.refs_0_), channel_id=1, source_target_pairs={{0,1},{1,0},{2,3},{3,2},{4,5},{5,4},{6,7},{7,6},{8,9},{9,8},{10,11... | collective-permute-start | bytes 1572872 | tf_op jit(solution)/shard_map/ppermute | solution.py:115
  (6 other events, 27.5 us)
